TPU v7x, 32 devices: a whole 2x2x4 slice. The times are simulated.
32 devices in a mesh: tmpl: 2 (over core), row: 4 (over z), col: 4 (over y, x).
Axes of the slice: x: 2, y: 2, z: 4, core: 2. Of those that a mesh axis runs over, the one named last changes fastest.
Arguments:
- template_pair: bfloat16 [2, 512, 64, 512], P('tmpl', 'row', None, 'col'), may hold values from -6 to 6
- trunk: bfloat16 [512, 128, 512], P('row', None, 'col'), may hold values from -6 to 6
- coverage: int32 [2, 512], replicated, may hold values from 0 to 1, as said below
- chain_ids: int32 [512], replicated, may hold values from 0 to 3, never falling along the last dimension, each value on 1 to 256 neighbouring positions
- chain_vec: float32 [64], replicated, may hold values from -4 to 4
- trunk_weights: bfloat16 [64, 128], replicated, may hold values from -0.5 to 0.5
- proj_weights: bfloat16 [2, 5, 64, 64], replicated, may hold values from -0.75 to 0.75
- out_weights: bfloat16 [2, 64, 64], replicated, may hold values from -0.75 to 0.75
- final_weights: bfloat16 [128, 64], replicated, may hold values from -0.75 to 0.75
Outputs:
- trunk_out: bfloat16 [512, 128, 512], P('row', None, 'col')
Inputs may be any that keep to these rules, and one draw needn't show every extreme that they name: coverage[t, i] is 1 where template t covers token i, else 0; how densely a template covers tokens is drawn anew for each block of 128 consecutive tokens. `chain_ids`: chain ids never fall along the tokens.
All inputs are finite; a program needn't handle non-finite values.
Results may differ from a plain program's by a relative error of at most 0.008.
Values may be sent and summed in bfloat16 or wider, within the bound.
No kernel may reach another device: no remote copies, remote signals or barrier semaphores. Data moves between devices by JAX's collectives and lax.ppermute only.
A program may use at most 128 MiB of HBM per device.

v0:
```python
import jax
import jax.numpy as jnp
from jax import lax
from jax.sharding import PartitionSpec as P

epsilon = 1e-05


def from_root(block, axis, source):
    block = jnp.where(lax.axis_index(axis) == source, block, jnp.zeros_like(block))
    return lax.psum(block, axis)


def channel_norm(values):
    centre = jnp.mean(values, axis=1, keepdims=True)
    centred = values - centre
    spread = jnp.mean(centred * centred, axis=1, keepdims=True)
    return centred * lax.rsqrt(spread + epsilon)


def project(weights, values):
    return jnp.einsum("dc,icj->idj", weights, values, preferred_element_type=jnp.float32)


def rounded(values):
    return lax.optimization_barrier(values.astype(jnp.bfloat16)).astype(jnp.float32)


def gated_pair(pair_rep, pair_mask, weights):
    channels = pair_rep.shape[1]
    normed = channel_norm(pair_rep.astype(jnp.float32)).astype(jnp.bfloat16)
    stacked = project(weights.reshape(5 * channels, channels), normed)
    pieces = [stacked[:, number * channels : (number + 1) * channels, :] for number in range(5)]
    weighted = pair_mask[:, None, :]
    left_proj = (weighted * jax.nn.sigmoid(pieces[0]) * pieces[1]).astype(jnp.bfloat16)
    right_proj = (weighted * jax.nn.sigmoid(pieces[2]) * pieces[3]).astype(jnp.bfloat16)
    return (left_proj, right_proj, pieces[4])


def apply_update(pair_rep, tri_sum, gate_proj, weights):
    tri_norm = channel_norm(tri_sum).astype(jnp.bfloat16)
    update = jax.nn.sigmoid(gate_proj) * project(weights, tri_norm)
    return (pair_rep.astype(jnp.float32) + update).astype(jnp.bfloat16)


def outgoing(left_proj, right_proj):
    right_cols = lax.all_gather(right_proj, "row", axis=0, tiled=True)
    partial_value = jnp.einsum(
        "ick,jck->icj", left_proj, right_cols, preferred_element_type=jnp.float32
    )
    return lax.psum_scatter(
        partial_value.astype(jnp.bfloat16), "col", scatter_dimension=2, tiled=True
    ).astype(jnp.float32)


def incoming(left_proj, right_proj):
    tile_rows, channels, tile_cols = left_proj.shape
    row_devices = lax.axis_size("row")
    owners = row_devices // lax.axis_size("col")
    left_cols, right_cols = (
        lax.all_gather(left_proj, "row", axis=0, tiled=True),
        lax.all_gather(right_proj, "row", axis=0, tiled=True),
    )
    offset = lax.axis_index("row") % owners * tile_rows
    column_piece = lax.dynamic_slice_in_dim(left_cols, offset, tile_rows, 2)
    left_mine = from_root(column_piece, "col", lax.axis_index("row") // owners)
    left_split = left_mine.reshape(row_devices, tile_rows, channels, tile_rows)
    right_split = right_cols.reshape(row_devices, tile_rows, channels, tile_cols)
    blocks = jnp.einsum(
        "gkci,gkcj->gicj", left_split, right_split, preferred_element_type=jnp.float32
    )
    return jnp.sum(rounded(blocks), axis=0)


def finish(trunk, pooled, cover_count, final_weights):
    hidden = jax.nn.relu(pooled / jnp.maximum(cover_count, 1.0)[:, None, :]).astype(jnp.bfloat16)
    return (trunk.astype(jnp.float32) + project(final_weights, hidden)).astype(jnp.bfloat16)


def per_device(
    template_pair,
    trunk,
    coverage,
    chain_ids,
    chain_vec,
    trunk_weights,
    proj_weights,
    out_weights,
    final_weights,
):
    tile_rows, trunk_channels, tile_cols = trunk.shape
    row_start = lax.axis_index("row") * tile_rows
    col_start = lax.axis_index("col") * tile_cols
    cover_float = coverage.astype(jnp.float32)
    cover_rows = lax.dynamic_slice_in_dim(cover_float, row_start, tile_rows, 1)
    cover_cols = lax.dynamic_slice_in_dim(cover_float, col_start, tile_cols, 1)
    cover_count = jnp.sum(cover_rows[:, :, None] * cover_cols[:, None, :], axis=0)
    chain_rows = lax.dynamic_slice_in_dim(chain_ids, row_start, tile_rows, 0)
    chain_cols = lax.dynamic_slice_in_dim(chain_ids, col_start, tile_cols, 0)
    same_chain = (chain_rows[:, None] == chain_cols[None, :]).astype(jnp.float32)
    trunk_proj = project(trunk_weights, channel_norm(trunk.astype(jnp.float32)))
    local_templates = template_pair.shape[0]
    template_index = lax.axis_index("tmpl") * local_templates + 0
    mask_rows = lax.dynamic_index_in_dim(cover_rows, template_index, 0, keepdims=False)
    mask_cols = lax.dynamic_index_in_dim(cover_cols, template_index, 0, keepdims=False)
    pair_mask = mask_rows[:, None] * mask_cols[None, :]
    pair_rep = (
        template_pair[0].astype(jnp.float32)
        + same_chain[:, None, :] * chain_vec[None, :, None]
        + trunk_proj
    ).astype(jnp.bfloat16)
    left_proj, right_proj, gate_proj = gated_pair(pair_rep, pair_mask, proj_weights[0])
    pair_rep = apply_update(pair_rep, outgoing(left_proj, right_proj), gate_proj, out_weights[0])
    left_proj, right_proj, gate_proj = gated_pair(pair_rep, pair_mask, proj_weights[1])
    pair_rep = apply_update(pair_rep, incoming(left_proj, right_proj), gate_proj, out_weights[1])
    pooled = pair_mask[:, None, :] * channel_norm(pair_rep.astype(jnp.float32))
    pooled_all = lax.psum(pooled.astype(jnp.bfloat16), "tmpl").astype(jnp.float32)
    return finish(trunk, pooled_all, cover_count, final_weights)


def solution(mesh):
    in_specs = (
        P("tmpl", "row", None, "col"),
        P("row", None, "col"),
        P(),
        P(),
        P(),
        P(),
        P(),
        P(),
        P(),
    )
    out_specs = P("row", None, "col")
    return jax.shard_map(
        per_device, mesh=mesh, in_specs=in_specs, out_specs=out_specs, check_vma=False
    )
```

profile of v0, /device:TPU:0, one launch (start us, length us, event | category | flops | bytes accessed | tf_op | source)
XLA Modules:
  0.0 877.8 jit_solution(267695753060939710)
XLA Ops:
  6.5 0.8 fusion.84
  7.4 6.4 copy.107
  13.7 3.5 convert_reduce_fusion.2
  17.3 4.8 fusion.2
  22.2 6.3 convert_reduce_fusion.4
  28.6 0.9 fusion.24
  29.6 8.5 convolution_bitcast_fusion.1
  38.3 8.4 fusion.47
  46.7 0.6 reduce-scatter.2.cloned.1.call-start
  47.3 151.9 %all-gather.4.cloned.1.call-done = bf16[512,64,128]{2,1,0:T(8,128)(2,1)} async-done(((bf16[128,64,128]{2,1,0:T(8,128)(2,1)}), bf16[512,64,128]{2,1,0:T(8,128)(2,1)}) %all-gather.4.cloned.1.call-update) | async-done | bytes 8388624 | tf_op jit(solution)/shard_map/all_gather | solution.py:47
  199.2 15.7 %convert_bitcast_fusion.1 = bf16[128,64,512]{0,2,1:T(8,128)(2,1)} fusion(bf16[512,64,128]{2,1,0:T(8,128)(2,1)} %all-gather.4.cloned.1.call-done, bf16[128,64,128]{2,1,0:T(8,128)(2,1)S(1)} %get-tuple-element.9), kind=kOutput, calls=%fused_computation.17 | convolution fusion | flops 1077936128 | bytes 18874368 | tf_op jit(solution)/shard_map/ick,jck->icj/dot_general | solution.py:48
  214.9 0.2 all-gather.8.cloned.1.call-start
  215.1 84.4 %reduce-scatter.2.cloned.1.call-done = bf16[128,64,128]{0,2,1:T(8,128)(2,1)} async-done(((bf16[128,64,512]{0,2,1:T(8,128)(2,1)}), bf16[128,64,128]{0,2,1:T(8,128)(2,1)}) %reduce-scatter.2.cloned.1.call-update) | async-done | bytes 2097168 | tf_op jit(solution)/shard_map/reduce_scatter | solution.py:51
  299.6 2.1 convert_reduce_fusion.6
  301.6 0.1 copy.112
  301.7 0.1 copy.113
  301.8 2.2 fusion.29
  304.0 0.1 copy.114
  304.1 0.1 copy.115
  304.2 2.0 fusion.30
  306.2 4.3 copy.116
  310.5 4.8 convert_reduce_fusion.3
  315.4 1.0 fusion.22
  316.4 2.9 convolution_bitcast_fusion
  319.3 4.4 fusion.38
  323.7 3.8 copy-done.1
  327.6 0.5 all-gather.6.cloned.1.call-update
  328.1 0.3 all-reduce.3.cloned.1.call-start
  328.4 148.9 %all-gather.8.cloned.1.call-done = bf16[512,64,128]{2,1,0:T(8,128)(2,1)} async-done(((bf16[128,64,128]{2,1,0:T(8,128)(2,1)}), bf16[512,64,128]{2,1,0:T(8,128)(2,1)}) %all-gather.8.cloned.1.call-update) | async-done | bytes 8388624 | tf_op jit(solution)/shard_map/all_gather | solution.py:61
  477.3 7.4 broadcast_select_fusion
  484.7 12.9 %copy.118 = bf16[4,128,64,128]{3,1,2,0:T(8,128)(2,1)} copy(bf16[4,128,64,128]{3,2,1,0:T(8,128)(2,1)} %bitcast.56) | data formatting | bytes 16777216 | tf_op jit(solution)/shard_map/reshape | solution.py:67
  497.6 0.3 all-reduce.5.cloned.1.call-start
  497.9 128.6 %all-gather.6.cloned.1.call-done = bf16[512,64,128]{2,1,0:T(8,128)(2,1)} async-done(((bf16[128,64,128]{2,1,0:T(8,128)(2,1)}), bf16[512,64,128]{2,1,0:T(8,128)(2,1)}) %all-gather.6.cloned.1.call-update) | async-done | bytes 8388624 | tf_op jit(solution)/shard_map/all_gather | solution.py:62
  626.5 173.6 %all-reduce.3.cloned.1.call-done = bf16[4,128,64,128]{3,1,2,0:T(8,128)(2,1)} async-done(((bf16[4,128,64,128]{3,1,2,0:T(8,128)(2,1)}), bf16[4,128,64,128]{3,1,2,0:T(8,128)(2,1)}) %all-reduce.3.cloned.1.call-update) | async-done | bytes 8388624 | tf_op jit(solution)/shard_map/psum | solution.py:11
  800.2 10.6 %convert_bitcast_fusion = bf16[4,128,64,128]{1,3,2,0:T(8,128)(2,1)S(1)} fusion(bf16[4,128,64,128]{3,1,2,0:T(8,128)(2,1)} %all-reduce.3.cloned.1.call-done, bf16[4,128,64,128]{3,2,1,0:T(8,128)(2,1)} %bitcast.57), kind=kOutput, calls=%fused_computation.16 | convolution fusion | flops 1077936128 | bytes 25165824 | tf_op jit(solution)/shard_map/gkci,gkcj->gicj/dot_general | solution.py:69
  810.7 5.0 convert_reduce_fusion
  815.9 0.1 copy.121
  815.9 2.6 multiply_reduce_fusion
  818.7 0.1 copy.123
  818.8 4.4 multiply_convert_fusion
  823.2 4.4 copy.124
  827.6 4.8 convert_reduce_fusion.5
  832.5 1.0 fusion.26
  833.5 2.3 fusion.28
  835.8 0.1 multiply_reduce_fusion.1
  835.9 22.0 %all-reduce.5.cloned.1.call-done = bf16[128,64,128]{2,1,0:T(8,128)(2,1)} async-done(((bf16[128,64,128]{2,1,0:T(8,128)(2,1)}), bf16[128,64,128]{2,1,0:T(8,128)(2,1)}) %all-reduce.5.cloned.1.call-update) | async-done | bytes 2097168 | tf_op jit(solution)/shard_map/psum | solution.py:117
  857.9 6.2 fusion.5
  864.1 6.4 copy.125
  (55 shorter events, 0.8 us)
Async XLA Ops:
  6.5 851.4 %copy-start = (bf16[128,64]{0,1:T(8,128)(2,1)S(1)}, bf16[128,64]{0,1:T(8,128)(2,1)}, u32[]{:S(2)}) copy-start(bf16[128,64]{0,1:T(8,128)(2,1)} %param.17) | copy-start | bytes 49156
  6.5 192.7 %all-gather.4.cloned.1.call-start = ((), (), s32[]{:S(2)}) async-start(), calls=%async_computation.1 | async-start | bytes 10485760 | tf_op jit(solution)/shard_map/all_gather | solution.py:47
  13.7 3.5 copy-start.2
  13.7 8.4 copy-start.10
  13.7 8.5 copy-start.12
  13.7 8.5 copy-start.13
  22.2 7.3 copy-start.8
  22.2 7.3 copy-start.9
  28.5 9.5 %copy-start.4 = (bf16[128,64,128]{2,1,0:T(8,128)(2,1)}, bf16[128,64,128]{2,1,0:T(8,128)(2,1)S(1)}, u32[]{:S(2)}) copy-start(bf16[128,64,128]{2,1,0:T(8,128)(2,1)S(1)} %get-tuple-element.20) | copy-start | bytes 6291460
  46.7 252.9 %reduce-scatter.2.cloned.1.call-start = ((), (), s32[]{:S(2)}) async-start(), calls=%async_computation.2 | async-start | bytes 10485760 | tf_op jit(solution)/shard_map/reduce_scatter | solution.py:51
  214.9 262.4 %all-gather.8.cloned.1.call-start = ((), (), s32[]{:S(2)}) async-start(), calls=%async_computation.4 | async-start | bytes 10485760 | tf_op jit(solution)/shard_map/all_gather | solution.py:61
  299.6 4.6 copy-start.3
  304.2 6.3 copy-start.11
  306.2 4.3 copy-start.5
  315.3 3.9 copy-start.6
  319.3 8.2 copy-start.1
  327.5 299.0 %all-gather.6.cloned.1.call-start = ((), (), s32[]{:S(2)}) async-start(), calls=%async_computation.3 | async-start | bytes 10485760 | tf_op jit(solution)/shard_map/all_gather | solution.py:62
  328.1 472.1 %all-reduce.3.cloned.1.call-start = ((), (), s32[]{:S(2)}) async-start(), calls=%async_computation.5 | async-start | bytes 16777216 | tf_op jit(solution)/shard_map/psum | solution.py:11
  497.6 360.3 %all-reduce.5.cloned.1.call-start = ((), (), s32[]{:S(2)}) async-start(), calls=%async_computation.6 | async-start | bytes 4194304 | tf_op jit(solution)/shard_map/psum | solution.py:117
  818.8 8.8 %copy-start.7 = (bf16[128,64,128]{2,1,0:T(8,128)(2,1)S(1)}, bf16[128,64,128]{2,1,0:T(8,128)(2,1)}, u32[]{:S(2)}) copy-start(bf16[128,64,128]{2,1,0:T(8,128)(2,1)} %copy-done.6) | copy-start | bytes 6291460
Sparse Core Ops, SparseCore 0:
  46.8 152.3 all-gather.3
  215.0 84.4 reduce-scatter.1
  327.7 149.5 all-gather.7
  478.7 147.7 all-gather.5
  629.9 170.2 all-reduce.2
  835.9 21.9 all-reduce.4
where the time goes:
time: 884 us; the launch traced here: 878 us
  waiting for transfers between devices  710 us (80%)
  matrix products  59.8 us (7%)
  other arithmetic  52.4 us (6%)
  local copies, waits for them, and re-layouts  39.8 us (5%)
  between operations  14.4 us (2%)
    psum x1, waiting for transfers between devices, from_root(): return lax.psum(block, axis)  174 us
    all_gather x1, waiting for transfers between devices, outgoing(): right_cols = lax.all_gather(right_proj, 'row', axis=0, tiled=True)  152 us
    all_gather x1, waiting for transfers between devices, incoming(): lax.all_gather(left_proj, 'row', axis=0, tiled=True)  149 us
    all_gather x1, waiting for transfers between devices, incoming(): lax.all_gather(right_proj, 'row', axis=0, tiled=True)  129 us
    reduce_scatter x1, waiting for transfers between devices, outgoing(): lax.psum_scatter(partial_value.astype(jnp.bfloat16), 'col', scatter_dimen...  84.4 us
    dot_general x6, matrix products, project(): jnp.einsum('dc,icj->idj', weights, values, preferred_element_type=jnp.flo...  33.5 us
    psum x1, waiting for transfers between devices, per_device(): lax.psum(pooled.astype(jnp.bfloat16), 'tmpl').astype(jnp.float32)  22 us
  transfers between devices with their start and end apart: 6, of which 6 were waited for; matrix products, arithmetic and copies ran while one was open for 2% of the time, Pallas kernels for 0%

commit v1 on v0

--- a/solution.py
+++ b/solution.py
@@ -2,13 +2,14 @@
 import jax.numpy as jnp
 from jax import lax
 from jax.sharding import PartitionSpec as P
+from jax.lax import all_gather
 
 epsilon = 1e-05
 
 
 def from_root(block, axis, source):
     block = jnp.where(lax.axis_index(axis) == source, block, jnp.zeros_like(block))
-    return lax.psum(block, axis)
+    return jnp.sum(all_gather(block, axis), axis=0)
 
 
 def channel_norm(values):

time: 884 us -> 1020 us (1.15)
  waiting for transfers between devices: 710 us -> 834 us
  other arithmetic: 52.4 us -> 69.9 us
  local copies, waits for them, and re-layouts: 39.8 us -> 26.7 us
    all_gather x0 -> x1, waiting for transfers between devices: none -> 294 us  [from_root(): return jnp.sum(all_gather(block, axis), axis=0)]
    psum x1 -> x0, waiting for transfers between devices: 174 us -> none  [from_root(): return lax.psum(block, axis)]
    reduce_sum x0 -> x1, other arithmetic: none -> 17.9 us  [from_root(): return jnp.sum(all_gather(block, axis), axis=0)]
    reshape x1 -> x0, local copies, waits for them, and re-layouts: 12.9 us -> none  [incoming(): left_split = left_mine.reshape(row_devices, tile_rows, channels, tile_rows)]
where the time goes in v1:
time: 1020 us; the launch traced here: 1010 us
  waiting for transfers between devices  834 us (82%)
  other arithmetic  69.9 us (7%)
  matrix products  67.8 us (7%)
  local copies, waits for them, and re-layouts  26.7 us (3%)
  between operations  14.3 us (1%)
    all_gather x1, waiting for transfers between devices, from_root(): return jnp.sum(all_gather(block, axis), axis=0)  294 us
    all_gather x1, waiting for transfers between devices, outgoing(): right_cols = lax.all_gather(right_proj, 'row', axis=0, tiled=True)  152 us
    all_gather x1, waiting for transfers between devices, incoming(): lax.all_gather(left_proj, 'row', axis=0, tiled=True)  150 us
    all_gather x1, waiting for transfers between devices, incoming(): lax.all_gather(right_proj, 'row', axis=0, tiled=True)  133 us
    reduce_scatter x1, waiting for transfers between devices, outgoing(): lax.psum_scatter(partial_value.astype(jnp.bfloat16), 'col', scatter_dimen...  84.4 us
    dot_general x6, matrix products, project(): jnp.einsum('dc,icj->idj', weights, values, preferred_element_type=jnp.flo...  33.5 us
  transfers between devices with their start and end apart: 6, of which 6 were waited for; matrix products, arithmetic and copies ran while one was open for 2% of the time, Pallas kernels for 0%

profile of v1, /device:TPU:0, one launch (start us, length us, event | category | flops | bytes accessed | tf_op | source)
XLA Modules:
  0.0 1013.7 jit_solution(5860931529723378268)
XLA Ops:
  6.5 0.8 fusion.87
  7.4 6.4 copy.107
  13.7 3.5 convert_reduce_fusion.2
  17.3 4.8 fusion.2
  22.2 6.3 convert_reduce_fusion.4
  28.6 0.9 fusion.27
  29.6 8.5 convolution_bitcast_fusion.1
  38.3 8.4 fusion.50
  46.7 0.5 reduce-scatter.2.cloned.1.call-start
  47.2 152.0 %all-gather.6.cloned.1.call-done = bf16[512,64,128]{2,1,0:T(8,128)(2,1)} async-done(((bf16[128,64,128]{2,1,0:T(8,128)(2,1)}), bf16[512,64,128]{2,1,0:T(8,128)(2,1)}) %all-gather.6.cloned.1.call-update) | async-done | bytes 8388624 | tf_op jit(solution)/shard_map/all_gather | solution.py:48
  199.2 15.7 %convert_bitcast_fusion.1 = bf16[128,64,512]{0,2,1:T(8,128)(2,1)} fusion(bf16[512,64,128]{2,1,0:T(8,128)(2,1)} %all-gather.6.cloned.1.call-done, bf16[128,64,128]{2,1,0:T(8,128)(2,1)S(1)} %get-tuple-element.9), kind=kOutput, calls=%fused_computation.18 | convolution fusion | flops 1077936128 | bytes 18874368 | tf_op jit(solution)/shard_map/ick,jck->icj/dot_general | solution.py:49
  214.9 0.2 all-gather.10.cloned.1.call-start
  215.1 84.4 %reduce-scatter.2.cloned.1.call-done = bf16[128,64,128]{0,2,1:T(8,128)(2,1)} async-done(((bf16[128,64,512]{0,2,1:T(8,128)(2,1)}), bf16[128,64,128]{0,2,1:T(8,128)(2,1)}) %reduce-scatter.2.cloned.1.call-update) | async-done | bytes 2097168 | tf_op jit(solution)/shard_map/reduce_scatter | solution.py:52
  299.6 2.1 convert_reduce_fusion.6
  301.6 0.1 copy.112
  301.7 0.1 copy.113
  301.8 2.2 fusion.32
  304.0 0.1 copy.114
  304.1 0.1 copy.115
  304.2 2.0 fusion.33
  306.2 4.3 copy.116
  310.5 4.8 convert_reduce_fusion.3
  315.4 1.0 fusion.25
  316.4 2.9 convolution_bitcast_fusion
  319.3 4.4 fusion.41
  323.7 3.9 copy-done.1
  327.7 149.7 %all-gather.10.cloned.1.call-done = bf16[512,64,128]{2,1,0:T(8,128)(2,1)} async-done(((bf16[128,64,128]{2,1,0:T(8,128)(2,1)}), bf16[512,64,128]{2,1,0:T(8,128)(2,1)}) %all-gather.10.cloned.1.call-update) | async-done | bytes 8388624 | tf_op jit(solution)/shard_map/all_gather | solution.py:62
  477.3 7.1 broadcast_select_fusion
  484.6 0.5 all-gather.8.cloned.1.call-update
  485.1 0.3 all-reduce.2.cloned.1.call-start
  485.4 294.5 %all-gather.12.cloned.1.call-done = bf16[2048,64,128]{2,1,0:T(8,128)(2,1)} async-done(((bf16[512,64,128]{2,1,0:T(8,128)(2,1)}), bf16[2048,64,128]{2,1,0:T(8,128)(2,1)}) %all-gather.12.cloned.1.call-update) | async-done | bytes 33554448 | tf_op jit(solution)/shard_map/all_gather | solution.py:12
  779.8 17.9 %reduce_sum.146 = bf16[512,64,128]{2,1,0:T(8,128)(2,1)} reduce(bf16[4,512,64,128]{3,2,1,0:T(8,128)(2,1)} %bitcast.56, bf16[]{:T(256)} %constant.93.clone.1), dimensions={0}, to_apply=%region_9.10 | reduce | flops 12582912 | bytes 41943040 | tf_op jit(solution)/shard_map/reduce_sum | solution.py:12
  797.7 133.2 %all-gather.8.cloned.1.call-done = bf16[512,64,128]{2,1,0:T(8,128)(2,1)} async-done(((bf16[128,64,128]{2,1,0:T(8,128)(2,1)}), bf16[512,64,128]{2,1,0:T(8,128)(2,1)}) %all-gather.8.cloned.1.call-update) | async-done | bytes 8388624 | tf_op jit(solution)/shard_map/all_gather | solution.py:63
  930.9 18.5 %convert_bitcast_fusion = bf16[4,128,64,128]{1,3,2,0:T(8,128)(2,1)S(1)} fusion(bf16[4,128,64,128]{3,2,1,0:T(8,128)(2,1)} %bitcast.57, bf16[4,128,64,128]{3,2,1,0:T(8,128)(2,1)} %bitcast.58), kind=kOutput, calls=%fused_computation.17 | convolution fusion | flops 1077936128 | bytes 25165824 | tf_op jit(solution)/shard_map/gkci,gkcj->gicj/dot_general | solution.py:70
  949.4 5.1 convert_reduce_fusion
  954.6 0.1 copy.121
  954.7 2.6 multiply_reduce_fusion
  957.4 0.1 copy.122
  957.5 0.1 copy.123
  957.6 4.3 multiply_convert_fusion
  961.9 4.1 copy.124
  966.0 4.8 convert_reduce_fusion.5
  970.9 1.0 fusion.29
  971.9 2.3 fusion.31
  974.2 0.1 multiply_reduce_fusion.1
  974.3 19.5 %all-reduce.2.cloned.1.call-done = bf16[128,64,128]{2,1,0:T(8,128)(2,1)} async-done(((bf16[128,64,128]{2,1,0:T(8,128)(2,1)}), bf16[128,64,128]{2,1,0:T(8,128)(2,1)}) %all-reduce.2.cloned.1.call-update) | async-done | bytes 2097168 | tf_op jit(solution)/shard_map/psum | solution.py:118
  993.8 6.2 fusion.5
  1000.1 6.4 copy.125
  (55 shorter events, 0.7 us)
Async XLA Ops:
  6.5 987.3 %copy-start = (bf16[128,64]{0,1:T(8,128)(2,1)S(1)}, bf16[128,64]{0,1:T(8,128)(2,1)}, u32[]{:S(2)}) copy-start(bf16[128,64]{0,1:T(8,128)(2,1)} %param.17) | copy-start | bytes 49156
  6.5 192.7 %all-gather.6.cloned.1.call-start = ((), (), s32[]{:S(2)}) async-start(), calls=%async_computation.1 | async-start | bytes 10485760 | tf_op jit(solution)/shard_map/all_gather | solution.py:48
  13.7 3.5 copy-start.2
  13.7 8.4 copy-start.10
  13.7 8.5 copy-start.12
  13.7 8.5 copy-start.13
  22.2 7.3 copy-start.8
  22.2 7.3 copy-start.9
  28.5 9.5 copy-start.4
  46.7 252.9 %reduce-scatter.2.cloned.1.call-start = ((), (), s32[]{:S(2)}) async-start(), calls=%async_computation.2 | async-start | bytes 10485760 | tf_op jit(solution)/shard_map/reduce_scatter | solution.py:52
  214.9 262.4 %all-gather.10.cloned.1.call-start = ((), (), s32[]{:S(2)}) async-start(), calls=%async_computation.4 | async-start | bytes 10485760 | tf_op jit(solution)/shard_map/all_gather | solution.py:62
  299.6 4.6 copy-start.3
  304.2 6.3 copy-start.11
  306.2 4.3 copy-start.5
  315.3 3.9 copy-start.6
  319.3 8.3 copy-start.1
  327.6 452.2 %all-gather.12.cloned.1.call-start = ((), (), s32[]{:S(2)}) async-start(), calls=%async_computation.6 | async-start | bytes 41943040 | tf_op jit(solution)/shard_map/all_gather | solution.py:12
  484.5 446.4 %all-gather.8.cloned.1.call-start = ((), (), s32[]{:S(2)}) async-start(), calls=%async_computation.3 | async-start | bytes 10485760 | tf_op jit(solution)/shard_map/all_gather | solution.py:63
  485.1 508.7 %all-reduce.2.cloned.1.call-start = ((), (), s32[]{:S(2)}) async-start(), calls=%async_computation.5 | async-start | bytes 4194304 | tf_op jit(solution)/shard_map/psum | solution.py:118
  957.6 8.5 copy-start.7
Sparse Core Ops, SparseCore 0:
  46.8 152.3 all-gather.5
  215.0 84.4 reduce-scatter.1
  327.7 149.5 all-gather.9
  484.6 295.1 all-gather.11
  781.2 149.5 all-gather.7
  974.3 19.4 all-reduce.1
